TPU v7x, 32 devices: a whole 2x2x4 slice. The times are simulated.
32 devices in a mesh: groups: 2 (over y), seq: 8 (over z, x), vocab: 1, batch: 2 (over core).
Axes of the slice: x: 2, y: 2, z: 4, core: 2. Of those that a mesh axis runs over, the one named last changes fastest.
Arguments:
- queries: bfloat16 [4, 1536, 3584], P(('groups', 'vocab', 'batch'), 'seq'), parts along dimension 0, may hold values from -300 to 300
- keys: bfloat16 [4, 1536, 512], P(('groups', 'vocab', 'batch'), 'seq'), parts along dimension 0, may hold values from -10 to 10
- values: bfloat16 [4, 1536, 512], P(('groups', 'vocab', 'batch'), 'seq'), parts along dimension 0, may hold values from -24 to 24
- residual: bfloat16 [4, 1536, 3584], P(('groups', 'vocab', 'batch'), 'seq'), parts along dimension 0, may hold values from -2048 to 2048
- norm_gain: float32 [3584], replicated, may hold values from 0.5 to 1.5
Outputs:
- normed: bfloat16 [4, 1536, 3584], P(('groups', 'vocab', 'batch'), 'seq'), parts along dimension 0
There are 2 independent parts, one for each index of `groups`. A program takes and returns all parts, laid end to end along the dimension named above; an argument that names none is the same for every part. Nothing has to cross between parts.
All inputs are finite; a program needn't handle non-finite values.
Results may differ from a plain program's by a relative error of at most 0.0049.
Values may be sent and summed in bfloat16 or wider, within the bound.
A program may use at most 128 MiB of HBM per device.

v0:
```python
import math
import jax
import jax.numpy as jnp
from jax import lax
from jax.sharding import PartitionSpec as P

HEAD_WIDTH = 128
group_slots = 8
norm_eps = 1e-06


def attend_block(query_block, key_seen, value_seen, first_row):
    scores = jnp.einsum("qhd,kd->hqk", query_block, key_seen, preferred_element_type=jnp.float32)
    scores = scores * (1.0 / math.sqrt(query_block.shape[2]))
    query_pos = first_row + jnp.arange(query_block.shape[0])
    key_pos = jnp.arange(key_seen.shape[0])
    allowed = key_pos[None, :] <= query_pos[:, None]
    scores = jnp.where(allowed[None], scores, -jnp.inf)
    row_max = jnp.max(scores, axis=2, keepdims=True)
    weights = jnp.exp(scores - row_max)
    soft_probs = (weights / jnp.sum(weights, axis=2, keepdims=True)).astype(jnp.bfloat16)
    output = jnp.einsum("hqk,kd->qhd", soft_probs, value_seen, preferred_element_type=jnp.float32)
    return output.astype(jnp.bfloat16)


def body(queries, keys, values, residual, norm_gain):
    seq_count = lax.axis_size("seq")
    seq_rows = queries.shape[1]
    total_rows = seq_rows * seq_count
    kv_heads = keys.shape[2] // HEAD_WIDTH
    q_heads = queries.shape[2] // HEAD_WIDTH
    queries_per_group = q_heads // kv_heads
    padded = kv_heads * group_slots
    local_heads = padded // seq_count
    query_rows = queries[0].reshape(seq_rows, kv_heads, queries_per_group, HEAD_WIDTH)
    query_pad = jnp.pad(
        query_rows, ((0, 0), (0, 0), (0, group_slots - queries_per_group), (0, 0))
    ).reshape(seq_rows, padded * HEAD_WIDTH)
    key_rows = keys[0].reshape(seq_rows, kv_heads, HEAD_WIDTH)
    value_rows = values[0].reshape(seq_rows, kv_heads, HEAD_WIDTH)
    key_send = jnp.repeat(key_rows, seq_count // kv_heads, axis=1).reshape(
        seq_rows, seq_count * HEAD_WIDTH
    )
    value_send = jnp.repeat(value_rows, seq_count // kv_heads, axis=1).reshape(
        seq_rows, seq_count * HEAD_WIDTH
    )
    query_here, key_here, value_here = (
        lax.all_to_all(query_pad, "seq", split_axis=1, concat_axis=0, tiled=True),
        lax.all_to_all(key_send, "seq", split_axis=1, concat_axis=0, tiled=True),
        lax.all_to_all(value_send, "seq", split_axis=1, concat_axis=0, tiled=True),
    )
    query_here = query_here.reshape(total_rows, local_heads, HEAD_WIDTH)
    block_rows = 512
    outputs = []
    for block_index in range(total_rows // block_rows):
        first_row = block_index * block_rows
        last_row = first_row + block_rows
        outputs.append(
            attend_block(
                query_here[first_row:last_row],
                key_here[:last_row],
                value_here[:last_row],
                first_row,
            )
        )
    attended = jnp.concatenate(outputs, axis=0).reshape(total_rows, local_heads * HEAD_WIDTH)
    returned = lax.all_to_all(attended, "seq", split_axis=0, concat_axis=1, tiled=True)
    attention = returned.reshape(seq_rows, kv_heads, group_slots, HEAD_WIDTH)[
        :, :, :queries_per_group
    ].reshape(seq_rows, q_heads * HEAD_WIDTH)
    hidden = residual[0].astype(jnp.float32) + attention.astype(jnp.float32)
    inv_rms = lax.rsqrt(jnp.mean(hidden * hidden, axis=1, keepdims=True) + norm_eps)
    normed = (hidden * inv_rms * norm_gain).astype(jnp.bfloat16)
    return normed[None]


def solution(mesh):
    return jax.shard_map(
        body,
        mesh=mesh,
        in_specs=(
            P(("groups", "vocab", "batch"), "seq", None),
            P(("groups", "vocab", "batch"), "seq", None),
            P(("groups", "vocab", "batch"), "seq", None),
            P(("groups", "vocab", "batch"), "seq", None),
            P(),
        ),
        out_specs=P(("groups", "vocab", "batch"), "seq", None),
        check_vma=False,
    )
```

profile of v0, /device:TPU:0, one launch (start us, length us, event | category | flops | bytes accessed | tf_op | source)
XLA Modules:
  0.0 180.9 jit_solution(12698471071452616194)
XLA Ops:
  0.0 3.1 %reshape_squeeze.9 = bf16[192,4,7,128]{3,2,1,0:T(8,128)(2,1)S(1)} reshape(bf16[1,192,3584]{2,1,0:T(8,128)(2,1)} %param.5) | data formatting | bytes 2752512 | tf_op jit(solution)/shard_map/reshape;squeeze | solution.py:35
  3.1 0.3 pad.4
  3.4 0.0 copy-start.5
  3.4 1.0 all_to_all.52
  4.4 0.0 copy-start.6
  4.5 1.6 copy.17
  6.1 7.3 %all-to-all-start = ((bf16[192,8,512]{2,0,1:T(8,128)(2,1)}), bf16[192,8,512]{2,0,1:T(8,128)(2,1)S(1)}, u32[]{:S(2)}, u32[]{:S(2)}) async-start(bf16[192,8,512]{2,0,1:T(8,128)(2,1)} %copy.17), calls=%async_computation | async-start | bytes 3145728 | tf_op jit(solution)/shard_map/all_to_all | solution.py:48
  13.4 0.1 reshape_squeeze.10
  13.5 0.0 copy-done.6
  13.5 0.1 reshape_squeeze.11
  13.5 0.7 copy.20
  14.2 0.8 iota_compare_fusion.2
  15.1 1.2 iota_compare_fusion.1
  16.2 34.2 %all-to-all-done = bf16[192,8,512]{2,0,1:T(8,128)(2,1)S(1)} async-done(((bf16[192,8,512]{2,0,1:T(8,128)(2,1)}), bf16[192,8,512]{2,0,1:T(8,128)(2,1)S(1)}, u32[]{:S(2)}, u32[]{:S(2)}) %all-to-all-start) | async-done | bytes 1572896 | tf_op jit(solution)/shard_map/all_to_all | solution.py:48
  50.4 0.8 broadcast_in_dim.41
  51.2 3.6 %all-to-all-start.1 = ((bf16[192,8,128]{2,0,1:T(8,128)(2,1)}), bf16[192,8,128]{2,0,1:T(8,128)(2,1)S(1)}, u32[]{:S(2)}, u32[]{:S(2)}) async-start(bf16[192,8,128]{2,0,1:T(8,128)(2,1)} %bitcast.1), calls=%async_computation.1 | async-start | bytes 786432 | tf_op jit(solution)/shard_map/all_to_all | solution.py:49
  54.8 1.4 iota_compare_fusion
  56.2 0.4 reshape.129
  56.6 0.5 fusion.58
  57.2 0.0 copy-start.4
  57.2 9.5 %all-to-all-done.1 = bf16[192,8,128]{2,0,1:T(8,128)(2,1)S(1)} async-done(((bf16[192,8,128]{2,0,1:T(8,128)(2,1)}), bf16[192,8,128]{2,0,1:T(8,128)(2,1)S(1)}, u32[]{:S(2)}, u32[]{:S(2)}) %all-to-all-start.1) | async-done | bytes 393248 | tf_op jit(solution)/shard_map/all_to_all | solution.py:49
  66.7 1.8 broadcast_in_dim.43
  68.4 3.6 %all-to-all-start.2 = ((bf16[192,8,128]{2,0,1:T(8,128)(2,1)}), bf16[192,8,128]{2,0,1:T(8,128)(2,1)S(1)}, u32[]{:S(2)}, u32[]{:S(2)}) async-start(bf16[192,8,128]{2,0,1:T(8,128)(2,1)} %bitcast.6), calls=%async_computation.2 | async-start | bytes 786432 | tf_op jit(solution)/shard_map/all_to_all | solution.py:50
  72.1 0.7 fusion.43
  72.8 3.9 %fusion.65 = (f32[4,512]{1,0:T(4,128)S(1)}, f32[4,512,512]{1,2,0:T(8,128)}) fusion(f32[512,4,512]{0,2,1:T(8,128)S(1)} %fusion.43, pred[512,512]{0,1:T(8,128)(4,1)S(1)} %copy-done.4), kind=kOutput, calls=%fused_computation.76 | output fusion | flops 6291967 | bytes 8658944 | tf_op jit(solution)/shard_map/sub | solution.py:20
  76.7 5.3 %fusion.60 = (f32[4,512]{1,0:T(4,128)S(1)}, f32[4,512,1024]{2,1,0:T(8,128)}) fusion(pred[512,1024]{1,0:T(8,128)(4,1)S(1)} %copy-done.3, bf16[512,4,128]{2,1,0:T(4,128)(2,1)S(1)} %get-tuple-element.6, bf16[1536,128]{1,0:T(8,128)(2,1)S(1)} %bitcast.87), kind=kOutput, calls=%fused_computation.75 | convolution fusion | flops 545260544 | bytes 9707520 | tf_op jit(solution)/shard_map/sub | solution.py:20
  82.0 1.8 %all-to-all-done.2 = bf16[192,8,128]{2,0,1:T(8,128)(2,1)S(1)} async-done(((bf16[192,8,128]{2,0,1:T(8,128)(2,1)}), bf16[192,8,128]{2,0,1:T(8,128)(2,1)S(1)}, u32[]{:S(2)}, u32[]{:S(2)}) %all-to-all-start.2) | async-done | bytes 393248 | tf_op jit(solution)/shard_map/all_to_all | solution.py:50
  83.8 3.1 %fusion.38 = bf16[512,4,128]{2,0,1:T(8,128)(2,1)S(1)} fusion(f32[4,512,512]{1,2,0:T(8,128)} %get-tuple-element.13, f32[4,512]{1,0:T(4,128)S(1)} %get-tuple-element.12, bf16[1536,128]{1,0:T(8,128)(2,1)S(1)} %bitcast.89), kind=kOutput, calls=%fused_computation.50 | convolution fusion | flops 270794752 | bytes 4857856 | tf_op jit(solution)/shard_map/hqk,kd->qhd/dot_general | solution.py:22
  87.0 1.5 copy-done.8
  88.5 1.4 fusion.37
  89.8 0.0 copy-start.2
  89.9 6.4 %fusion.41 = f32[512,4,1536]{2,0,1:T(8,128)} fusion(bf16[1536,128,1]{1,0,2:T(8,128)(2,1)S(1)} %bitcast.88, bf16[512,4,128]{2,1,0:T(4,128)(2,1)S(1)} %get-tuple-element.7), kind=kOutput, calls=%fused_computation.53 | convolution fusion | flops 805306368 | bytes 13500416 | tf_op jit(solution)/shard_map/qhd,kd->hqk/dot_general | solution.py:13
  96.2 0.0 copy-done.2
  96.2 16.0 %fusion.59 = (f32[4,512]{1,0:T(4,128)S(1)}, f32[4,512,1536]{2,1,0:T(8,128)}) fusion(f32[512,4,1536]{2,0,1:T(8,128)} %fusion.41, pred[512,1536]{1,0:T(8,128)(4,1)S(1)} %copy-done.2), kind=kOutput, calls=%fused_computation.74 | output fusion | flops 18875904 | bytes 25960448 | tf_op jit(solution)/shard_map/sub | solution.py:20
  112.2 6.4 %fusion.36 = bf16[512,4,128]{2,0,1:T(8,128)(2,1)S(1)} fusion(bf16[1536,128,1]{1,0,2:T(8,128)(2,1)S(1)} %bitcast.91, f32[4,512,1536]{2,1,0:T(8,128)} %get-tuple-element.9, f32[4,512]{1,0:T(4,128)S(1)} %get-tuple-element.8), kind=kOutput, calls=%fused_computation.48 | convolution fusion | flops 811859968 | bytes 13508608 | tf_op jit(solution)/shard_map/hqk,kd->qhd/dot_general | solution.py:22
  118.6 0.1 pad_maximum_fusion
  118.7 7.3 %copy.24 = bf16[1536,4,128]{2,1,0:T(4,128)(2,1)S(1)} copy(bf16[1536,4,128]{2,0,1:T(8,128)(2,1)S(1)} %pad_maximum_fusion) | data formatting | bytes 3145728 | tf_op jit(solution)/shard_map/concatenate | solution.py:66
  126.1 0.6 all_to_all.63
  126.7 40.6 %all_to_all.70 = bf16[8,192,512]{2,1,0:T(8,128)(2,1)S(1)} all-to-all(bf16[8,192,512]{2,1,0:T(8,128)(2,1)S(1)} %all_to_all.63), channel_id=1, replica_groups=mesh['groups'=2,'seq'=8,'vocab'=1,'batch'=2] {'seq'}, dimensions={0} | all-to-all | bytes 3145728 | tf_op jit(solution)/shard_map/all_to_all | solution.py:67
  167.3 0.9 copy.25
  168.2 2.3 %reshape.130 = bf16[192,4,8,128]{3,2,1,0:T(8,128)(2,1)} reshape(bf16[192,8,512]{2,1,0:T(8,128)(2,1)S(1)} %copy.25) | data formatting | bytes 3145728 | tf_op jit(solution)/shard_map/reshape | solution.py:68
  170.4 1.8 %slice_convert_fusion = f32[192,4,7,128]{3,2,1,0:T(8,128)S(1)} fusion(bf16[192,4,8,128]{3,2,1,0:T(8,128)(2,1)} %reshape.130), kind=kLoop, calls=%fused_computation.43 | loop fusion | flops 688128 | bytes 4128768 | tf_op jit(solution)/shard_map/convert_element_type | solution.py:71
  172.3 1.9 %reshape.133 = f32[192,3584]{1,0:T(8,128)} reshape(f32[192,4,7,128]{3,2,1,0:T(8,128)S(1)} %slice_convert_fusion) | data formatting | bytes 5505024 | tf_op jit(solution)/shard_map/convert_element_type | solution.py:71
  174.1 1.8 %reshape.131 = f32[1,192,3584]{2,1,0:T(8,128)} reshape(f32[192,4,7,128]{3,2,1,0:T(8,128)S(1)} %slice_convert_fusion) | data formatting | bytes 5505024 | tf_op jit(solution)/shard_map/convert_element_type | solution.py:71
  175.9 2.8 %fusion.28 = f32[192]{0:T(256)S(1)} fusion(f32[192,3584]{1,0:T(8,128)} %reshape.133, bf16[1,192,3584]{2,1,0:T(8,128)(2,1)} %param.8), kind=kLoop, calls=%fused_computation.37 | loop fusion | flops 2752320 | bytes 4129536 | tf_op jit(solution)/shard_map/reduce_sum | solution.py:72
  178.7 0.2 copy-done
  179.0 0.4 copy-done.1
  179.4 1.6 fusion.25
  (13 shorter events, 0.1 us)
Async XLA Ops:
  3.4 10.0 %copy-start.5 = (bf16[1,192,512]{2,1,0:T(8,128)(2,1)S(1)}, bf16[1,192,512]{2,1,0:T(8,128)(2,1)}, u32[]{:S(2)}) copy-start(bf16[1,192,512]{2,1,0:T(8,128)(2,1)} %param.6) | copy-start | bytes 589828
  4.4 9.0 %copy-start.6 = (bf16[1,192,512]{2,1,0:T(8,128)(2,1)S(1)}, bf16[1,192,512]{2,1,0:T(8,128)(2,1)}, u32[]{:S(2)}) copy-start(bf16[1,192,512]{2,1,0:T(8,128)(2,1)} %param.7) | copy-start | bytes 589828
  6.1 44.3 %all-to-all-start = ((bf16[192,8,512]{2,0,1:T(8,128)(2,1)}), bf16[192,8,512]{2,0,1:T(8,128)(2,1)S(1)}, u32[]{:S(2)}, u32[]{:S(2)}) async-start(bf16[192,8,512]{2,0,1:T(8,128)(2,1)} %copy.17), calls=%async_computation | async-start | bytes 3145728 | tf_op jit(solution)/shard_map/all_to_all | solution.py:48
  51.2 15.5 %all-to-all-start.1 = ((bf16[192,8,128]{2,0,1:T(8,128)(2,1)}), bf16[192,8,128]{2,0,1:T(8,128)(2,1)S(1)}, u32[]{:S(2)}, u32[]{:S(2)}) async-start(bf16[192,8,128]{2,0,1:T(8,128)(2,1)} %bitcast.1), calls=%async_computation.1 | async-start | bytes 786432 | tf_op jit(solution)/shard_map/all_to_all | solution.py:49
  57.2 15.6 %copy-start.4 = (pred[512,512]{0,1:T(8,128)(4,1)S(1)}, pred[512,512]{0,1:T(8,128)(4,1)}, u32[]{:S(2)}) copy-start(pred[512,512]{0,1:T(8,128)(4,1)} %iota_compare_fusion.2) | copy-start | bytes 786436
  68.4 15.4 %all-to-all-start.2 = ((bf16[192,8,128]{2,0,1:T(8,128)(2,1)}), bf16[192,8,128]{2,0,1:T(8,128)(2,1)S(1)}, u32[]{:S(2)}, u32[]{:S(2)}) async-start(bf16[192,8,128]{2,0,1:T(8,128)(2,1)} %bitcast.6), calls=%async_computation.2 | async-start | bytes 786432 | tf_op jit(solution)/shard_map/all_to_all | solution.py:50
  72.8 4.0 %copy-start.3 = (pred[512,1024]{1,0:T(8,128)(4,1)S(1)}, pred[512,1024]{1,0:T(8,128)(4,1)}, u32[]{:S(2)}) copy-start(pred[512,1024]{1,0:T(8,128)(4,1)} %iota_compare_fusion.1) | copy-start | bytes 1572868
  83.8 4.6 %copy-start.8 = (f32[4,512,1024]{2,1,0:T(8,128)S(1)}, f32[4,512,1024]{2,1,0:T(8,128)}, u32[]{:S(2)}) copy-start(f32[4,512,1024]{2,1,0:T(8,128)} %get-tuple-element.11) | copy-start | bytes 25165828
  89.8 6.4 %copy-start.2 = (pred[512,1536]{1,0:T(8,128)(4,1)S(1)}, pred[512,1536]{1,0:T(8,128)(4,1)}, u32[]{:S(2)}) copy-start(pred[512,1536]{1,0:T(8,128)(4,1)} %iota_compare_fusion) | copy-start | bytes 2359300
  174.1 4.6 %copy-start.7 = (f32[3584]{0:T(1024)S(1)}, f32[3584]{0:T(1024)}, u32[]{:S(2)}) copy-start(f32[3584]{0:T(1024)} %param.9) | copy-start | bytes 43012
  175.9 3.0 %copy-start = (f32[1,192,3584]{2,1,0:T(8,128)S(1)}, f32[1,192,3584]{2,1,0:T(8,128)}, u32[]{:S(2)}) copy-start(f32[1,192,3584]{2,1,0:T(8,128)} %reshape.131) | copy-start | bytes 8257540
  175.9 3.4 %copy-start.1 = (bf16[1,192,3584]{2,1,0:T(8,128)(2,1)S(1)}, bf16[1,192,3584]{2,1,0:T(8,128)(2,1)}, u32[]{:S(2)}) copy-start(bf16[1,192,3584]{2,1,0:T(8,128)(2,1)} %param.8) | copy-start | bytes 4128772
where the time goes:
time: 181 us
  waiting for transfers between devices  45.5 us (25%)
  blocking collectives  40.6 us (22%)
  other arithmetic  29.5 us (16%)
  local copies, waits for them, and re-layouts  27.3 us (15%)
  matrix products  23.3 us (13%)
  starting transfers between devices  14.6 us (8%)
    all_to_all x1, blocking collectives, body(): lax.all_to_all(attended, 'seq', split_axis=0, concat_axis=1, tiled=True)  40.6 us
    all_to_all x1, waiting for transfers between devices, body(): lax.all_to_all(query_pad, 'seq', split_axis=1, concat_axis=0, tiled=True)  34.2 us
    sub x2, other arithmetic, attend_block(): weights = jnp.exp(scores - row_max)  19.9 us
    dot_general x3, matrix products, attend_block(): jnp.einsum('hqk,kd->qhd', soft_probs, value_seen, preferred_element_type=...  10.9 us
    all_to_all x1, waiting for transfers between devices, body(): lax.all_to_all(key_send, 'seq', split_axis=1, concat_axis=0, tiled=True)  9.5 us
    concatenate x1, local copies, waits for them, and re-layouts, body(): jnp.concatenate(outputs, axis=0)  7.33 us
    all_to_all x1, starting transfers between devices, body(): lax.all_to_all(query_pad, 'seq', split_axis=1, concat_axis=0, tiled=True)  7.28 us
    dot_general x2, matrix products, attend_block(): jnp.einsum('qhd,kd->hqk', query_block, key_seen, preferred_element_type=j...  7.08 us
  transfers between devices with their start and end apart: 3, of which 3 were waited for; matrix products, arithmetic and copies ran while one was open for 8% of the time, Pallas kernels for 0%

commit v1 on v0

--- a/solution.py
+++ b/solution.py
@@ -7,6 +7,13 @@
 HEAD_WIDTH = 128
 group_slots = 8
 norm_eps = 1e-06
+
+
+def trade_parts(shard, axis, split, join):
+    devices = lax.axis_size(axis)
+    blocks = jnp.stack(jnp.split(shard, devices, axis=split), axis=0)
+    blocks = lax.all_to_all(blocks, axis, split_axis=0, concat_axis=0)
+    return jnp.concatenate(blocks, axis=join)
 
 
 def attend_block(query_block, key_seen, value_seen, first_row):
@@ -46,7 +53,7 @@
     )
     query_here, key_here, value_here = (
         lax.all_to_all(query_pad, "seq", split_axis=1, concat_axis=0, tiled=True),
-        lax.all_to_all(key_send, "seq", split_axis=1, concat_axis=0, tiled=True),
+        trade_parts(key_send, "seq", 1, 0),
         lax.all_to_all(value_send, "seq", split_axis=1, concat_axis=0, tiled=True),
     )
     query_here = query_here.reshape(total_rows, local_heads, HEAD_WIDTH)

time: 181 us -> 171 us (0.945)
  waiting for transfers between devices: 45.5 us -> 38.1 us
  other arithmetic: 29.5 us -> 22.7 us
  local copies, waits for them, and re-layouts: 27.3 us -> 33 us
  matrix products: 23.3 us -> 20.6 us
    sub x2, other arithmetic: 19.9 us -> 13 us  [attend_block(): weights = jnp.exp(scores - row_max)]
    all_to_all x1, waiting for transfers between devices: 34.2 us -> 28.6 us  [body(): lax.all_to_all(query_pad, 'seq', split_axis=1, concat_axis=0, tiled=True)]
    dot_general x2, matrix products: 7.08 us -> 2.51 us  [attend_block(): jnp.einsum('qhd,kd->hqk', query_block, key_seen, preferred_element_type=j...]
    unnamed x18 -> x33, local copies, waits for them, and re-layouts: 2.19 us -> 6.68 us
  transfers between devices with their start and end apart: 3 -> 3, of which waited for: 3 -> 3; matrix products, arithmetic and copies ran while one was open for 8% -> 13% of each run, Pallas kernels for 0% -> 0%
where the time goes in v1:
time: 171 us
  blocking collectives  41.5 us (24%)
  waiting for transfers between devices  38.1 us (22%)
  local copies, waits for them, and re-layouts  33 us (19%)
  other arithmetic  22.7 us (13%)
  matrix products  20.6 us (12%)
  starting transfers between devices  14.6 us (9%)
    all_to_all x1, blocking collectives, body(): lax.all_to_all(attended, 'seq', split_axis=0, concat_axis=1, tiled=True)  41.5 us
    all_to_all x1, waiting for transfers between devices, body(): lax.all_to_all(query_pad, 'seq', split_axis=1, concat_axis=0, tiled=True)  28.6 us
    sub x2, other arithmetic, attend_block(): weights = jnp.exp(scores - row_max)  13 us
    dot_general x3, matrix products, attend_block(): jnp.einsum('hqk,kd->qhd', soft_probs, value_seen, preferred_element_type=...  11.9 us
    all_to_all x1, waiting for transfers between devices, trade_parts(): blocks = lax.all_to_all(blocks, axis, split_axis=0, concat_axis=0)  8.61 us
    concatenate x1, local copies, waits for them, and re-layouts, body(): jnp.concatenate(outputs, axis=0)  7.33 us
    all_to_all x1, starting transfers between devices, body(): lax.all_to_all(query_pad, 'seq', split_axis=1, concat_axis=0, tiled=True)  7.28 us
    unnamed x33, local copies, waits for them, and re-layouts  6.68 us
  transfers between devices with their start and end apart: 3, of which 3 were waited for; matrix products, arithmetic and copies ran while one was open for 13% of the time, Pallas kernels for 0%

profile of v1, /device:TPU:0, one launch (start us, length us, event | category | flops | bytes accessed | tf_op | source)
XLA Modules:
  0.0 170.7 jit_solution(5237182241310677727)
XLA Ops:
  0.0 3.1 %reshape_squeeze.10 = bf16[192,4,7,128]{3,2,1,0:T(8,128)(2,1)S(1)} reshape(bf16[1,192,3584]{2,1,0:T(8,128)(2,1)} %param.5) | data formatting | bytes 2752512 | tf_op jit(solution)/shard_map/reshape;squeeze | solution.py:42
  3.1 0.3 pad.4
  3.4 1.0 all_to_all.42
  4.5 1.7 copy.19
  6.1 7.3 %all-to-all-start.1 = ((bf16[192,8,512]{2,0,1:T(8,128)(2,1)}), bf16[192,8,512]{2,0,1:T(8,128)(2,1)S(1)}, u32[]{:S(2)}, u32[]{:S(2)}) async-start(bf16[192,8,512]{2,0,1:T(8,128)(2,1)} %copy.19), calls=%async_computation.1 | async-start | bytes 3145728 | tf_op jit(solution)/shard_map/all_to_all | solution.py:55
  13.5 0.3 broadcast_in_dim.41
  13.7 0.3 reshape_reshape.4
  14.1 0.7 copy.21
  14.8 0.8 iota_compare_fusion.2
  15.6 0.6 fusion.50
  16.2 0.6 fusion.49
  16.8 0.6 fusion.48
  17.5 0.6 fusion.47
  18.1 0.6 fusion.46
  18.7 0.6 fusion.45
  19.3 0.6 fusion.44
  20.0 0.6 fusion.43
  20.6 1.2 iota_compare_fusion.1
  21.8 28.6 %all-to-all-done.1 = bf16[192,8,512]{2,0,1:T(8,128)(2,1)S(1)} async-done(((bf16[192,8,512]{2,0,1:T(8,128)(2,1)}), bf16[192,8,512]{2,0,1:T(8,128)(2,1)S(1)}, u32[]{:S(2)}, u32[]{:S(2)}) %all-to-all-start.1) | async-done | bytes 1572896 | tf_op jit(solution)/shard_map/all_to_all | solution.py:55
  50.4 3.6 %all-to-all-start = ((bf16[8,192,128]{2,1,0:T(8,128)(2,1)}), bf16[8,192,128]{2,1,0:T(8,128)(2,1)S(1)}, u32[]{:S(2)}, u32[]{:S(2)}) async-start(bf16[8,192,128]{2,1,0:T(8,128)(2,1)} %fusion.43), calls=%async_computation | async-start | bytes 786432 | tf_op jit(solution)/shard_map/all_to_all | solution.py:15
  54.0 1.5 iota_compare_fusion
  55.5 0.4 reshape.129
  55.9 1.4 fusion.57
  57.3 8.6 %all-to-all-done = bf16[8,192,128]{2,1,0:T(8,128)(2,1)S(1)} async-done(((bf16[8,192,128]{2,1,0:T(8,128)(2,1)}), bf16[8,192,128]{2,1,0:T(8,128)(2,1)S(1)}, u32[]{:S(2)}, u32[]{:S(2)}) %all-to-all-start) | async-done | bytes 393248 | tf_op jit(solution)/shard_map/all_to_all | solution.py:15
  65.9 1.8 %broadcast_in_dim.43 = bf16[192,4,2,128]{3,0,2,1:T(8,128)(2,1)} broadcast(bf16[192,4,128]{2,0,1:T(8,128)(2,1)} %copy.21), dimensions={0,1,3} | broadcast | bytes 589824 | tf_op jit(solution)/shard_map/broadcast_in_dim | solution.py:51
  67.7 3.6 %all-to-all-start.2 = ((bf16[192,8,128]{2,0,1:T(8,128)(2,1)}), bf16[192,8,128]{2,0,1:T(8,128)(2,1)S(1)}, u32[]{:S(2)}, u32[]{:S(2)}) async-start(bf16[192,8,128]{2,0,1:T(8,128)(2,1)} %bitcast.12), calls=%async_computation.2 | async-start | bytes 786432 | tf_op jit(solution)/shard_map/all_to_all | solution.py:57
  71.3 0.7 fusion.34
  72.0 3.9 %fusion.64 = (f32[4,512]{1,0:T(4,128)S(1)}, f32[4,512,512]{1,2,0:T(8,128)}) fusion(f32[512,512,4]{1,0,2:T(8,128)S(1)} %fusion.34, pred[512,512]{0,1:T(8,128)(4,1)S(1)} %copy-done.8), kind=kOutput, calls=%fused_computation.86 | output fusion | flops 6291967 | bytes 8658944 | tf_op jit(solution)/shard_map/sub | solution.py:27
  76.0 6.3 %fusion.59 = (f32[4,512]{1,0:T(4,128)S(1)}, f32[4,512,1024]{1,2,0:T(8,128)}) fusion(pred[512,1024]{0,1:T(8,128)(4,1)S(1)} %copy-done.4, bf16[512,4,128]{2,1,0:T(4,128)(2,1)S(1)} %get-tuple-element.6, bf16[1536,128]{1,0:T(8,128)(2,1)S(1)} %bitcast.116), kind=kOutput, calls=%fused_computation.85 | convolution fusion | flops 545260544 | bytes 9707520 | tf_op jit(solution)/shard_map/sub | solution.py:27
  82.2 0.9 all-to-all-done.2
  83.1 3.2 %fusion.29 = bf16[512,4,128]{2,0,1:T(8,128)(2,1)S(1)} fusion(f32[4,512,512]{1,2,0:T(8,128)} %get-tuple-element.13, f32[4,512]{1,0:T(4,128)S(1)} %get-tuple-element.12, bf16[1536,128]{1,0:T(8,128)(2,1)S(1)} %bitcast.118), kind=kOutput, calls=%fused_computation.44 | convolution fusion | flops 270794752 | bytes 4857856 | tf_op jit(solution)/shard_map/hqk,kd->qhd/dot_general | solution.py:29
  86.3 1.6 copy-done.12
  87.9 2.2 %fusion.28 = bf16[512,4,128]{2,0,1:T(8,128)(2,1)} fusion(f32[4,512,1024]{1,2,0:T(8,128)S(1)} %copy-done.12, f32[4,512]{1,0:T(4,128)S(1)} %get-tuple-element.10, bf16[1536,128]{1,0:T(8,128)(2,1)S(1)} %bitcast.119), kind=kOutput, calls=%fused_computation.43 | convolution fusion | flops 541327360 | bytes 9183232 | tf_op jit(solution)/shard_map/hqk,kd->qhd/dot_general | solution.py:29
  90.1 1.8 %fusion.32 = f32[1536,512,4]{1,0,2:T(8,128)S(1)} fusion(bf16[1536,128,1]{1,0,2:T(8,128)(2,1)S(1)} %bitcast.117, bf16[512,4,128]{2,1,0:T(4,128)(2,1)S(1)} %copy-done.2), kind=kOutput, calls=%fused_computation.47 | convolution fusion | flops 805306368 | bytes 13500416 | tf_op jit(solution)/shard_map/qhd,kd->hqk/dot_general | solution.py:20
  91.9 9.0 %fusion.58 = (f32[4,512]{1,0:T(4,128)S(1)}, f32[4,512,1536]{1,2,0:T(8,128)}) fusion(f32[1536,512,4]{1,0,2:T(8,128)S(1)} %fusion.32, pred[512,1536]{0,1:T(8,128)(4,1)S(1)} %copy-done.3), kind=kOutput, calls=%fused_computation.84 | output fusion | flops 18875904 | bytes 25960448 | tf_op jit(solution)/shard_map/sub | solution.py:27
  101.0 6.5 %fusion.27 = bf16[512,4,128]{2,0,1:T(8,128)(2,1)S(1)} fusion(bf16[1536,128,1]{1,0,2:T(8,128)(2,1)S(1)} %bitcast.120, f32[4,512,1536]{1,2,0:T(8,128)} %get-tuple-element.9, f32[4,512]{1,0:T(4,128)S(1)} %get-tuple-element.8), kind=kOutput, calls=%fused_computation.42 | convolution fusion | flops 811859968 | bytes 13508608 | tf_op jit(solution)/shard_map/hqk,kd->qhd/dot_general | solution.py:29
  107.6 7.3 %copy.27 = bf16[1536,4,128]{2,1,0:T(4,128)(2,1)S(1)} copy(bf16[1536,4,128]{2,0,1:T(8,128)(2,1)S(1)} %pad_maximum_fusion) | data formatting | bytes 3145728 | tf_op jit(solution)/shard_map/concatenate | solution.py:73
  114.9 0.6 all_to_all.49
  115.6 41.5 %all_to_all.56 = bf16[8,192,512]{2,1,0:T(8,128)(2,1)S(1)} all-to-all(bf16[8,192,512]{2,1,0:T(8,128)(2,1)S(1)} %all_to_all.49), channel_id=1, replica_groups=mesh['groups'=2,'seq'=8,'vocab'=1,'batch'=2] {'seq'}, dimensions={0} | all-to-all | bytes 3145728 | tf_op jit(solution)/shard_map/all_to_all | solution.py:74
  157.1 0.9 copy.28
  158.0 2.2 %reshape.130 = bf16[192,4,8,128]{3,2,1,0:T(8,128)(2,1)} reshape(bf16[192,8,512]{2,1,0:T(8,128)(2,1)S(1)} %copy.28) | data formatting | bytes 3145728 | tf_op jit(solution)/shard_map/reshape | solution.py:75
  160.2 1.8 %slice_convert_fusion = f32[192,4,7,128]{3,2,1,0:T(8,128)S(1)} fusion(bf16[192,4,8,128]{3,2,1,0:T(8,128)(2,1)} %reshape.130), kind=kLoop, calls=%fused_computation.37 | loop fusion | flops 688128 | bytes 4128768 | tf_op jit(solution)/shard_map/convert_element_type | solution.py:78
  162.1 1.9 %reshape.133 = f32[192,3584]{1,0:T(8,128)} reshape(f32[192,4,7,128]{3,2,1,0:T(8,128)S(1)} %slice_convert_fusion) | data formatting | bytes 5505024 | tf_op jit(solution)/shard_map/convert_element_type | solution.py:78
  163.9 1.8 %reshape.131 = f32[1,192,3584]{2,1,0:T(8,128)} reshape(f32[192,4,7,128]{3,2,1,0:T(8,128)S(1)} %slice_convert_fusion) | data formatting | bytes 5505024 | tf_op jit(solution)/shard_map/convert_element_type | solution.py:78
  165.8 2.8 %fusion.19 = f32[192]{0:T(256)S(1)} fusion(f32[192,3584]{1,0:T(8,128)} %reshape.133, bf16[1,192,3584]{2,1,0:T(8,128)(2,1)} %param.8), kind=kLoop, calls=%fused_computation.31 | loop fusion | flops 2752320 | bytes 4129536 | tf_op jit(solution)/shard_map/reduce_sum | solution.py:79
  168.5 0.2 copy-done
  168.8 0.4 copy-done.1
  169.2 1.6 fusion.16
  (29 shorter events, 0.3 us)
Async XLA Ops:
  3.4 10.0 %copy-start.9 = (bf16[1,192,512]{2,1,0:T(8,128)(2,1)S(1)}, bf16[1,192,512]{2,1,0:T(8,128)(2,1)}, u32[]{:S(2)}) copy-start(bf16[1,192,512]{2,1,0:T(8,128)(2,1)} %param.6) | copy-start | bytes 589828
  4.4 9.6 %copy-start.10 = (bf16[1,192,512]{2,1,0:T(8,128)(2,1)S(1)}, bf16[1,192,512]{2,1,0:T(8,128)(2,1)}, u32[]{:S(2)}) copy-start(bf16[1,192,512]{2,1,0:T(8,128)(2,1)} %param.7) | copy-start | bytes 589828
  6.1 44.3 %all-to-all-start.1 = ((bf16[192,8,512]{2,0,1:T(8,128)(2,1)}), bf16[192,8,512]{2,0,1:T(8,128)(2,1)S(1)}, u32[]{:S(2)}, u32[]{:S(2)}) async-start(bf16[192,8,512]{2,0,1:T(8,128)(2,1)} %copy.19), calls=%async_computation.1 | async-start | bytes 3145728 | tf_op jit(solution)/shard_map/all_to_all | solution.py:55
  50.4 15.5 %all-to-all-start = ((bf16[8,192,128]{2,1,0:T(8,128)(2,1)}), bf16[8,192,128]{2,1,0:T(8,128)(2,1)S(1)}, u32[]{:S(2)}, u32[]{:S(2)}) async-start(bf16[8,192,128]{2,1,0:T(8,128)(2,1)} %fusion.43), calls=%async_computation | async-start | bytes 786432 | tf_op jit(solution)/shard_map/all_to_all | solution.py:15
  57.3 14.7 %copy-start.8 = (pred[512,512]{0,1:T(8,128)(4,1)S(1)}, pred[512,512]{0,1:T(8,128)(4,1)}, u32[]{:S(2)}) copy-start(pred[512,512]{0,1:T(8,128)(4,1)} %iota_compare_fusion.2) | copy-start | bytes 786436
  67.7 15.4 %all-to-all-start.2 = ((bf16[192,8,128]{2,0,1:T(8,128)(2,1)}), bf16[192,8,128]{2,0,1:T(8,128)(2,1)S(1)}, u32[]{:S(2)}, u32[]{:S(2)}) async-start(bf16[192,8,128]{2,0,1:T(8,128)(2,1)} %bitcast.12), calls=%async_computation.2 | async-start | bytes 786432 | tf_op jit(solution)/shard_map/all_to_all | solution.py:57
  72.0 3.9 %copy-start.4 = (pred[512,1024]{0,1:T(8,128)(4,1)S(1)}, pred[512,1024]{0,1:T(8,128)(4,1)}, u32[]{:S(2)}) copy-start(pred[512,1024]{0,1:T(8,128)(4,1)} %iota_compare_fusion.1) | copy-start | bytes 1572868
  83.1 3.2 %copy-start.6 = (bf16[192,8,128]{2,0,1:T(8,128)(2,1)}, bf16[192,8,128]{2,0,1:T(8,128)(2,1)S(1)}, u32[]{:S(2)}) copy-start(bf16[192,8,128]{2,0,1:T(8,128)(2,1)S(1)} %all-to-all-done.2) | copy-start | bytes 1179652
  83.1 4.8 %copy-start.12 = (f32[4,512,1024]{1,2,0:T(8,128)S(1)}, f32[4,512,1024]{1,2,0:T(8,128)}, u32[]{:S(2)}) copy-start(f32[4,512,1024]{1,2,0:T(8,128)} %get-tuple-element.11) | copy-start | bytes 25165828
  87.9 2.2 %copy-start.2 = (bf16[512,4,128]{2,1,0:T(4,128)(2,1)S(1)}, bf16[512,4,128]{2,1,0:T(4,128)(2,1)}, u32[]{:S(2)}) copy-start(bf16[512,4,128]{2,1,0:T(4,128)(2,1)} %get-tuple-element.7) | copy-start | bytes 1572868
  90.1 1.8 %copy-start.3 = (pred[512,1536]{0,1:T(8,128)(4,1)S(1)}, pred[512,1536]{0,1:T(8,128)(4,1)}, u32[]{:S(2)}) copy-start(pred[512,1536]{0,1:T(8,128)(4,1)} %iota_compare_fusion) | copy-start | bytes 2359300
  91.9 9.0 %copy-start.7 = (bf16[192,8,128]{2,0,1:T(8,128)(2,1)S(1)}, bf16[192,8,128]{2,0,1:T(8,128)(2,1)}, u32[]{:S(2)}) copy-start(bf16[192,8,128]{2,0,1:T(8,128)(2,1)} %copy-done.6) | copy-start | bytes 1179652
  101.0 6.5 %copy-start.5 = (bf16[512,4,128]{2,0,1:T(8,128)(2,1)S(1)}, bf16[512,4,128]{2,0,1:T(8,128)(2,1)}, u32[]{:S(2)}) copy-start(bf16[512,4,128]{2,0,1:T(8,128)(2,1)} %fusion.28) | copy-start | bytes 1572868
  163.9 4.6 %copy-start.11 = (f32[3584]{0:T(1024)S(1)}, f32[3584]{0:T(1024)}, u32[]{:S(2)}) copy-start(f32[3584]{0:T(1024)} %param.9) | copy-start | bytes 43012
  165.8 3.0 %copy-start = (f32[1,192,3584]{2,1,0:T(8,128)S(1)}, f32[1,192,3584]{2,1,0:T(8,128)}, u32[]{:S(2)}) copy-start(f32[1,192,3584]{2,1,0:T(8,128)} %reshape.131) | copy-start | bytes 8257540
  165.8 3.4 %copy-start.1 = (bf16[1,192,3584]{2,1,0:T(8,128)(2,1)S(1)}, bf16[1,192,3584]{2,1,0:T(8,128)(2,1)}, u32[]{:S(2)}) copy-start(bf16[1,192,3584]{2,1,0:T(8,128)(2,1)} %param.8) | copy-start | bytes 4128772
